TPU v7x, 128 devices: a whole 4x4x4 slice. The times are simulated.
128 devices in a mesh: row: 8 (over z_hi, x), col: 16 (over z_lo, y, core).
Axes of the slice: x: 4, y: 4, z: 4 (z_hi: 2, z_lo: 2; z = z_hi * 2 + z_lo), core: 2. Of those that a mesh axis runs over, the one named last changes fastest.
Arguments:
- diag_blocks: float32 [2, 512, 512], replicated, may hold values from -1 to 5, as said below
- pivot_flags: int32 [2, 512], replicated, may hold values 0 or 1
- panels: bfloat16 [2, 32768, 512], P(None, ('row', 'col')), may hold values from -3 to 3
- structure: int32 [2, 32768], P(None, ('row', 'col')), may hold values 0 or 1
- ancestor_inverse: bfloat16 [32768, 32768], P('row', 'col'), may hold values from -0.046875 to 0.046875
Outputs:
- inverse_panel: bfloat16 [2, 32768, 512], P(None, ('row', 'col'))
- inverse_diagonal: float32 [2, 512, 512], replicated
Inputs may be any that keep to these rules, and one draw needn't show every extreme that they name: Each diag_blocks[k] is symmetric, and its off-diagonal part is small enough that every eigenvalue of each shifted block is at least 0.8, so every shifted block is positive definite.
All inputs are finite; a program needn't handle non-finite values. No bound on the sum of `structure` on one device may be relied on, other than what follows from the above.
Results may differ from a plain program's by a relative error of at most 0.0051.
Values may be sent and summed in bfloat16 or wider, within the bound.
No kernel may reach another device: no remote copies, remote signals or barrier semaphores. Data moves between devices by JAX's collectives and lax.ppermute only.
A program may use at most 192 MiB of HBM per device.

v0:
```python
import jax
import jax.numpy as jnp
from jax import lax
from jax.sharding import PartitionSpec as P

HIGHEST_PRECISION = lax.Precision.HIGHEST
PERTURBATION = 1.0


def from_root(value, axis, source):
    kept = jnp.where(lax.axis_index(axis) == source, value, 0).astype(value.dtype)
    return lax.psum(kept, axis)


def factor_inverse(diagonal_block, flag_row):
    node_width = diagonal_block.shape[0]
    identity = jnp.eye(node_width, dtype=jnp.float32)
    shifted = diagonal_block + PERTURBATION * identity * flag_row.astype(jnp.float32)[None, :]
    factor_lower = jnp.linalg.cholesky(shifted)
    lower_inverse = jax.scipy.linalg.solve_triangular(factor_lower, identity, lower=True)
    return jnp.dot(lower_inverse.T, lower_inverse, precision=HIGHEST_PRECISION)


def normalize_panel(panel_rows, member_row, inverse):
    masked = panel_rows.astype(jnp.float32) * member_row.astype(jnp.float32)[:, None]
    return jnp.dot(masked, inverse, precision=HIGHEST_PRECISION).astype(jnp.bfloat16)


def exact_contract(left_rows, right_rows):
    dims = (((0,), (0,)), ((), ()))
    return lax.dot_general(
        left_rows.astype(jnp.float32),
        right_rows,
        dims,
        precision=HIGHEST_PRECISION,
        preferred_element_type=jnp.float32,
    )


def local(diag_blocks, pivot_flags, panels, structure, ancestor_inverse):
    node_count = diag_blocks.shape[0]
    node_width = diag_blocks.shape[2]
    inverses = [
        factor_inverse(diag_blocks[supernode], pivot_flags[supernode])
        for supernode in range(node_count)
    ]
    normed = [
        normalize_panel(panels[supernode], structure[supernode], inverses[supernode])
        for supernode in range(node_count)
    ]
    groups = jnp.concatenate(normed, axis=1)
    col_ratio = lax.axis_size("col") // lax.axis_size("row")
    col_index = lax.axis_index("col")
    own_rows = ancestor_inverse.shape[0] // lax.axis_size("col")
    panel_terms = []
    diagonal_terms = []
    row_block = lax.all_gather(groups, "col", axis=0, tiled=True)
    block_rows = row_block.shape[0] // col_ratio
    column_part = lax.dynamic_slice_in_dim(
        row_block, col_index % col_ratio * block_rows, block_rows, 0
    )
    column_block = from_root(column_part, "row", col_index // col_ratio)
    group_size = groups.shape[1] // node_width

    def product(offset, row_count, column_block=column_block):
        return jnp.dot(ancestor_inverse, column_block, preferred_element_type=jnp.float32)

    summed = lax.psum_scatter(
        product(jnp.int32(0), own_rows * lax.axis_size("col")),
        "col",
        scatter_dimension=0,
        tiled=True,
    )
    for member in range(group_size):
        lower_col = member * node_width
        diagonal_terms.append(
            exact_contract(
                groups[:, lower_col : lower_col + node_width],
                summed[:, lower_col : lower_col + node_width],
            )
        )
    for member in range(group_size):
        lower_col = member * node_width
        panel_terms.append(summed[:, lower_col : lower_col + node_width])
    totals = lax.psum(jnp.stack(diagonal_terms), ("row", "col"))
    inverse_diagonal = jnp.stack(inverses) + totals
    inverse_panel = (-jnp.stack(panel_terms)).astype(jnp.bfloat16)
    return (inverse_panel, inverse_diagonal)


def solution(mesh):
    in_specs = (P(), P(), P(None, ("row", "col"), None), P(None, ("row", "col")), P("row", "col"))
    out_specs = (P(None, ("row", "col"), None), P())
    return jax.shard_map(local, mesh=mesh, in_specs=in_specs, out_specs=out_specs, check_vma=False)
```

profile of v0, /device:TPU:1, one launch (start us, length us, event | category | flops | bytes accessed | tf_op | source)
XLA Modules:
  0.0 775.6 jit_solution(5468474773533071747)
XLA Ops:
  19.6 11.7 %cholesky.358 = f32[128,128]{1,0:T(8,128)S(1)} custom-call(f32[128,128]{1,0:T(8,128)S(1)} %cholesky.439), custom_call_target="Cholesky" | custom-call | tf_op jit(solution)/shard_map/jit(cholesky)/cholesky | solution.py:19
  31.3 9.8 %custom-call.31 = f32[1,128,128]{1,2,0:T(8,128)S(1)} custom-call(f32[1,128,128]{2,1,0:T(8,128)S(1)} %get-tuple-element.65), custom_call_target="InvertDiagBlocksLowerTriangular" | custom-call | tf_op jit(solution)/shard_map/jit(cholesky)/cholesky | solution.py:19
  43.8 11.7 %cholesky.377 = f32[128,128]{1,0:T(8,128)S(1)} custom-call(f32[128,128]{1,0:T(8,128)S(1)} %cholesky.443), custom_call_target="Cholesky" | custom-call | tf_op jit(solution)/shard_map/jit(cholesky)/cholesky | solution.py:19
  55.6 10.0 %custom-call.32 = f32[1,128,128]{1,2,0:T(8,128)S(1)} custom-call(f32[1,128,128]{2,1,0:T(8,128)S(1)} %get-tuple-element.62), custom_call_target="InvertDiagBlocksLowerTriangular" | custom-call | tf_op jit(solution)/shard_map/jit(cholesky)/cholesky | solution.py:19
  67.1 11.7 %cholesky.398 = f32[128,128]{1,0:T(8,128)S(1)} custom-call(f32[128,128]{1,0:T(8,128)S(1)} %cholesky.448), custom_call_target="Cholesky" | custom-call | tf_op jit(solution)/shard_map/jit(cholesky)/cholesky | solution.py:19
  79.6 9.8 %custom-call.33 = f32[1,128,128]{1,2,0:T(8,128)S(1)} custom-call(f32[1,128,128]{2,1,0:T(8,128)S(1)} %get-tuple-element.59), custom_call_target="InvertDiagBlocksLowerTriangular" | custom-call | tf_op jit(solution)/shard_map/jit(cholesky)/cholesky | solution.py:19
  90.8 12.1 %cholesky.415 = f32[128,128]{1,0:T(8,128)S(1)} custom-call(f32[128,128]{1,0:T(8,128)S(1)} %convolution_subtract_fusion.10), custom_call_target="Cholesky" | custom-call | tf_op jit(solution)/shard_map/jit(cholesky)/cholesky | solution.py:19
  107.9 11.7 %while.5 = (s32[]{:T(128)}, f32[512,512]{1,0:T(8,128)}, s32[4,2]{0,1:T(2,128)S(1)}, f32[4,128,128]{2,1,0:T(8,128)S(1)}, s32[]{:T(128)}) while((s32[]{:T(128)}, f32[512,512]{1,0:T(8,128)}, s32[4,2]{0,1:T(2,128)S(1)}, f32[4,128,128]{2,1,0:T(8,128)S(1)}, s32[]{:T(128)}) %tuple.61), condition=%wide.while_cond.clone, body=%wide.while_body.clone.sunk | while | flops 2 | bytes 131189 | solution.py:20
  119.6 39.3 %custom-call.34 = f32[4,128,128]{1,2,0:T(8,128)S(1)} custom-call(f32[4,128,128]{2,1,0:T(8,128)S(1)} %get-tuple-element.19), custom_call_target="InvertDiagBlocksLowerTriangular" | custom-call | tf_op jit(solution)/shard_map/jit(_solve_triangular)/triangular_solve | solution.py:20
  172.3 11.7 %cholesky.286 = f32[128,128]{1,0:T(8,128)S(1)} custom-call(f32[128,128]{1,0:T(8,128)S(1)} %cholesky.426), custom_call_target="Cholesky" | custom-call | tf_op jit(solution)/shard_map/jit(cholesky)/cholesky | solution.py:19
  184.1 10.0 %custom-call.27 = f32[1,128,128]{1,2,0:T(8,128)S(1)} custom-call(f32[1,128,128]{2,1,0:T(8,128)S(1)} %get-tuple-element.55), custom_call_target="InvertDiagBlocksLowerTriangular" | custom-call | tf_op jit(solution)/shard_map/jit(cholesky)/cholesky | solution.py:19
  194.8 11.7 %cholesky.305 = f32[128,128]{1,0:T(8,128)S(1)} custom-call(f32[128,128]{1,0:T(8,128)S(1)} %cholesky.430), custom_call_target="Cholesky" | custom-call | tf_op jit(solution)/shard_map/jit(cholesky)/cholesky | solution.py:19
  206.6 9.8 %custom-call.28 = f32[1,128,128]{1,2,0:T(8,128)S(1)} custom-call(f32[1,128,128]{2,1,0:T(8,128)S(1)} %get-tuple-element.52), custom_call_target="InvertDiagBlocksLowerTriangular" | custom-call | tf_op jit(solution)/shard_map/jit(cholesky)/cholesky | solution.py:19
  217.1 11.7 %cholesky.326 = f32[128,128]{1,0:T(8,128)S(1)} custom-call(f32[128,128]{1,0:T(8,128)S(1)} %cholesky.435), custom_call_target="Cholesky" | custom-call | tf_op jit(solution)/shard_map/jit(cholesky)/cholesky | solution.py:19
  229.6 10.0 %custom-call.29 = f32[1,128,128]{1,2,0:T(8,128)S(1)} custom-call(f32[1,128,128]{2,1,0:T(8,128)S(1)} %get-tuple-element.49), custom_call_target="InvertDiagBlocksLowerTriangular" | custom-call | tf_op jit(solution)/shard_map/jit(cholesky)/cholesky | solution.py:19
  240.2 11.7 %cholesky.343 = f32[128,128]{1,0:T(8,128)S(1)} custom-call(f32[128,128]{1,0:T(8,128)S(1)} %convolution_subtract_fusion.11), custom_call_target="Cholesky" | custom-call | tf_op jit(solution)/shard_map/jit(cholesky)/cholesky | solution.py:19
  256.6 10.6 %while.4 = (s32[]{:T(128)}, f32[512,512]{1,0:T(8,128)S(1)}, s32[4,2]{0,1:T(2,128)S(1)}, f32[4,128,128]{2,1,0:T(8,128)}, s32[]{:T(128)}) while((s32[]{:T(128)}, f32[512,512]{1,0:T(8,128)S(1)}, s32[4,2]{0,1:T(2,128)S(1)}, f32[4,128,128]{2,1,0:T(8,128)}, s32[]{:T(128)}) %tuple.75), condition=%wide.while_cond, body=%wide.while_body.sunk | while | flops 2 | bytes 132205 | solution.py:20
  267.2 40.6 %custom-call.30 = f32[4,128,128]{1,2,0:T(8,128)S(1)} custom-call(f32[4,128,128]{2,1,0:T(8,128)} %get-tuple-element.18), custom_call_target="InvertDiagBlocksLowerTriangular" | custom-call | tf_op jit(solution)/shard_map/jit(_solve_triangular)/triangular_solve | solution.py:20
  317.7 55.8 %all-gather.2.cloned.1.call-done = bf16[4096,1024]{1,0:T(8,128)(2,1)} async-done(((bf16[256,1024]{1,0:T(8,128)(2,1)}), bf16[4096,1024]{1,0:T(8,128)(2,1)}) %all-gather.2.cloned.1.call-update) | async-done | bytes 8388624 | tf_op jit(solution)/shard_map/all_gather | solution.py:57
  373.5 5.4 dynamic-slice_select_fusion
  379.0 110.3 %all-reduce.4.cloned.1.call-done = bf16[2048,1024]{1,0:T(8,128)(2,1)} async-done(((bf16[2048,1024]{1,0:T(8,128)(2,1)}), bf16[2048,1024]{1,0:T(8,128)(2,1)}) %all-reduce.4.cloned.1.call-update) | async-done | bytes 4194320 | tf_op jit(solution)/shard_map/psum | solution.py:12
  489.3 23.8 %convolution_bitcast_fusion = f32[4096,1024]{0,1:T(8,128)} fusion(bf16[2048,1024]{1,0:T(8,128)(2,1)} %all-reduce.4.cloned.1.call-done, bf16[4096,2048]{1,0:T(8,128)(2,1)} %param.12), kind=kOutput, calls=%fused_computation.4 | convolution fusion | flops 17179869184 | bytes 37748736 | tf_op jit(solution)/shard_map/dot_general | solution.py:66
  513.1 95.7 %reduce-scatter.2.cloned.1.call-done = f32[256,1024]{0,1:T(8,128)} async-done(((f32[4096,1024]{0,1:T(8,128)}), f32[256,1024]{0,1:T(8,128)}) %reduce-scatter.2.cloned.1.call-update) | async-done | bytes 1048592 | tf_op jit(solution)/shard_map/reduce_scatter | solution.py:68
  615.2 150.4 %all-reduce.6.cloned.1.call-done = f32[2,512,512]{2,1,0:T(8,128)} async-done(((f32[2,512,512]{2,1,0:T(8,128)}), f32[2,512,512]{2,1,0:T(8,128)}) %all-reduce.6.cloned.1.call-update) | async-done | bytes 2097168 | tf_op jit(solution)/shard_map/psum | solution.py:85
  (118 shorter events, 81.3 us)
Async XLA Ops:
  7.2 366.4 %all-gather.2.cloned.1.call-start = ((), (), s32[]{:S(2)}) async-start(), calls=%async_computation.1 | async-start | bytes 8912896 | tf_op jit(solution)/shard_map/all_gather | solution.py:57
  18.6 1.0 copy-start.2
  267.2 47.4 %copy-start.1 = (f32[512,512]{1,0:T(8,128)S(1)}, f32[512,512]{1,0:T(8,128)}, u32[]{:S(2)}) copy-start(f32[512,512]{1,0:T(8,128)} %fusion.8) | copy-start | bytes 3145732
  307.8 6.8 copy-start.3
  317.7 171.6 %all-reduce.4.cloned.1.call-start = ((), (), s32[]{:S(2)}) async-start(), calls=%async_computation.2 | async-start | bytes 8388608 | tf_op jit(solution)/shard_map/psum | solution.py:12
  378.9 229.9 %reduce-scatter.2.cloned.1.call-start = ((), (), s32[]{:S(2)}) async-start(), calls=%async_computation.3 | async-start | bytes 17825792 | tf_op jit(solution)/shard_map/reduce_scatter | solution.py:68
  513.1 252.5 %all-reduce.6.cloned.1.call-start = ((), (), s32[]{:S(2)}) async-start(), calls=%async_computation.4 | async-start | bytes 4194304 | tf_op jit(solution)/shard_map/psum | solution.py:85
  610.6 3.4 copy-start
Sparse Core Ops, SparseCore 0:
  317.8 55.7 all-gather.1
  379.1 110.1 all-reduce.3
  513.2 95.6 reduce-scatter.1
  614.1 151.3 all-reduce.5
where the time goes:
time: 785 us; the launch traced here: 776 us
  waiting for transfers between devices  412 us (52%)
  other arithmetic  256 us (33%)
  matrix products  53.9 us (7%)
  local copies, waits for them, and re-layouts  33.7 us (4%)
  between operations  19.5 us (2%)
    another operation x28, other arithmetic, factor_inverse(): factor_lower = jnp.linalg.cholesky(shifted)  158 us
    psum x1, waiting for transfers between devices, local(): totals = lax.psum(jnp.stack(diagonal_terms), ('row', 'col'))  150 us
    psum x1, waiting for transfers between devices, from_root(): return lax.psum(kept, axis)  110 us
    reduce_scatter x1, waiting for transfers between devices, local(): lax.psum_scatter(product(jnp.int32(0), own_rows * lax.axis_size('col')),...  95.7 us
    another operation x5, other arithmetic, factor_inverse(): jax.scipy.linalg.solve_triangular(factor_lower, identity, lower=True)  81.2 us
    all_gather x1, waiting for transfers between devices, local(): row_block = lax.all_gather(groups, 'col', axis=0, tiled=True)  55.8 us
    dot_general x1, matrix products, product(): jnp.dot(ancestor_inverse, column_block, preferred_element_type=jnp.float32)  23.8 us
    another operation x27, local copies, waits for them, and re-layouts, factor_inverse(): jax.scipy.linalg.solve_triangular(factor_lower, identity, lower=True)  22.9 us
  transfers between devices with their start and end apart: 4, of which 4 were waited for; matrix products, arithmetic and copies ran while one was open for 0% of the time, Pallas kernels for 0%

commit v1 on v0

--- a/solution.py
+++ b/solution.py
@@ -54,7 +54,8 @@
     own_rows = ancestor_inverse.shape[0] // lax.axis_size("col")
     panel_terms = []
     diagonal_terms = []
-    row_block = lax.all_gather(groups, "col", axis=0, tiled=True)
+    repeated = jnp.stack([groups] * lax.axis_size("col"))
+    row_block = jnp.concatenate(lax.all_to_all(repeated, "col", 0, 0), axis=0)
     block_rows = row_block.shape[0] // col_ratio
     column_part = lax.dynamic_slice_in_dim(
         row_block, col_index % col_ratio * block_rows, block_rows, 0

time: 785 us -> 854 us (1.088)
  waiting for transfers between devices: 412 us -> 470 us
    all_to_all x0 -> x1, waiting for transfers between devices: none -> 112 us  [local(): row_block = jnp.concatenate(lax.all_to_all(repeated, 'col', 0, 0), axis=0)]
    all_gather x1 -> x0, waiting for transfers between devices: 55.8 us -> none  [local(): row_block = lax.all_gather(groups, 'col', axis=0, tiled=True)]
where the time goes in v1:
time: 854 us; the launch traced here: 844 us
  waiting for transfers between devices  470 us (55%)
  other arithmetic  255 us (30%)
  matrix products  53.9 us (6%)
  local copies, waits for them, and re-layouts  38 us (4%)
  between operations  19.5 us (2%)
    another operation x28, other arithmetic, factor_inverse(): factor_lower = jnp.linalg.cholesky(shifted)  158 us
    psum x1, waiting for transfers between devices, local(): totals = lax.psum(jnp.stack(diagonal_terms), ('row', 'col'))  151 us
    all_to_all x1, waiting for transfers between devices, local(): row_block = jnp.concatenate(lax.all_to_all(repeated, 'col', 0, 0), axis=0)  112 us
    psum x1, waiting for transfers between devices, from_root(): return lax.psum(kept, axis)  111 us
    reduce_scatter x1, waiting for transfers between devices, local(): lax.psum_scatter(product(jnp.int32(0), own_rows * lax.axis_size('col')),...  95.7 us
    another operation x5, other arithmetic, factor_inverse(): jax.scipy.linalg.solve_triangular(factor_lower, identity, lower=True)  81.2 us
    dot_general x1, matrix products, product(): jnp.dot(ancestor_inverse, column_block, preferred_element_type=jnp.float32)  23.8 us
    another operation x27, local copies, waits for them, and re-layouts, factor_inverse(): jax.scipy.linalg.solve_triangular(factor_lower, identity, lower=True)  22.9 us
  transfers between devices with their start and end apart: 4, of which 4 were waited for; matrix products, arithmetic and copies ran while one was open for 0% of the time, Pallas kernels for 0%

profile of v1, /device:TPU:1, one launch (start us, length us, event | category | flops | bytes accessed | tf_op | source)
XLA Modules:
  0.0 843.9 jit_solution(8605765310299673890)
XLA Ops:
  19.5 11.7 %cholesky.358 = f32[128,128]{1,0:T(8,128)S(1)} custom-call(f32[128,128]{1,0:T(8,128)S(1)} %cholesky.439), custom_call_target="Cholesky" | custom-call | tf_op jit(solution)/shard_map/jit(cholesky)/cholesky | solution.py:19
  31.3 9.8 %custom-call.31 = f32[1,128,128]{1,2,0:T(8,128)S(1)} custom-call(f32[1,128,128]{2,1,0:T(8,128)S(1)} %get-tuple-element.65), custom_call_target="InvertDiagBlocksLowerTriangular" | custom-call | tf_op jit(solution)/shard_map/jit(cholesky)/cholesky | solution.py:19
  43.8 11.7 %cholesky.377 = f32[128,128]{1,0:T(8,128)S(1)} custom-call(f32[128,128]{1,0:T(8,128)S(1)} %cholesky.443), custom_call_target="Cholesky" | custom-call | tf_op jit(solution)/shard_map/jit(cholesky)/cholesky | solution.py:19
  55.5 10.0 %custom-call.32 = f32[1,128,128]{1,2,0:T(8,128)S(1)} custom-call(f32[1,128,128]{2,1,0:T(8,128)S(1)} %get-tuple-element.62), custom_call_target="InvertDiagBlocksLowerTriangular" | custom-call | tf_op jit(solution)/shard_map/jit(cholesky)/cholesky | solution.py:19
  67.1 11.7 %cholesky.398 = f32[128,128]{1,0:T(8,128)S(1)} custom-call(f32[128,128]{1,0:T(8,128)S(1)} %cholesky.448), custom_call_target="Cholesky" | custom-call | tf_op jit(solution)/shard_map/jit(cholesky)/cholesky | solution.py:19
  79.5 9.8 %custom-call.33 = f32[1,128,128]{1,2,0:T(8,128)S(1)} custom-call(f32[1,128,128]{2,1,0:T(8,128)S(1)} %get-tuple-element.59), custom_call_target="InvertDiagBlocksLowerTriangular" | custom-call | tf_op jit(solution)/shard_map/jit(cholesky)/cholesky | solution.py:19
  90.8 12.1 %cholesky.415 = f32[128,128]{1,0:T(8,128)S(1)} custom-call(f32[128,128]{1,0:T(8,128)S(1)} %convolution_subtract_fusion.10), custom_call_target="Cholesky" | custom-call | tf_op jit(solution)/shard_map/jit(cholesky)/cholesky | solution.py:19
  107.8 11.7 %while.5 = (s32[]{:T(128)}, f32[512,512]{1,0:T(8,128)}, s32[4,2]{0,1:T(2,128)S(1)}, f32[4,128,128]{2,1,0:T(8,128)S(1)}, s32[]{:T(128)}) while((s32[]{:T(128)}, f32[512,512]{1,0:T(8,128)}, s32[4,2]{0,1:T(2,128)S(1)}, f32[4,128,128]{2,1,0:T(8,128)S(1)}, s32[]{:T(128)}) %tuple.61), condition=%wide.while_cond.clone, body=%wide.while_body.clone.sunk | while | flops 2 | bytes 131189 | solution.py:20
  119.5 39.3 %custom-call.34 = f32[4,128,128]{1,2,0:T(8,128)S(1)} custom-call(f32[4,128,128]{2,1,0:T(8,128)S(1)} %get-tuple-element.19), custom_call_target="InvertDiagBlocksLowerTriangular" | custom-call | tf_op jit(solution)/shard_map/jit(_solve_triangular)/triangular_solve | solution.py:20
  172.3 11.7 %cholesky.286 = f32[128,128]{1,0:T(8,128)S(1)} custom-call(f32[128,128]{1,0:T(8,128)S(1)} %cholesky.426), custom_call_target="Cholesky" | custom-call | tf_op jit(solution)/shard_map/jit(cholesky)/cholesky | solution.py:19
  184.0 10.0 %custom-call.27 = f32[1,128,128]{1,2,0:T(8,128)S(1)} custom-call(f32[1,128,128]{2,1,0:T(8,128)S(1)} %get-tuple-element.55), custom_call_target="InvertDiagBlocksLowerTriangular" | custom-call | tf_op jit(solution)/shard_map/jit(cholesky)/cholesky | solution.py:19
  194.8 11.7 %cholesky.305 = f32[128,128]{1,0:T(8,128)S(1)} custom-call(f32[128,128]{1,0:T(8,128)S(1)} %cholesky.430), custom_call_target="Cholesky" | custom-call | tf_op jit(solution)/shard_map/jit(cholesky)/cholesky | solution.py:19
  206.5 9.8 %custom-call.28 = f32[1,128,128]{1,2,0:T(8,128)S(1)} custom-call(f32[1,128,128]{2,1,0:T(8,128)S(1)} %get-tuple-element.52), custom_call_target="InvertDiagBlocksLowerTriangular" | custom-call | tf_op jit(solution)/shard_map/jit(cholesky)/cholesky | solution.py:19
  217.0 11.7 %cholesky.326 = f32[128,128]{1,0:T(8,128)S(1)} custom-call(f32[128,128]{1,0:T(8,128)S(1)} %cholesky.435), custom_call_target="Cholesky" | custom-call | tf_op jit(solution)/shard_map/jit(cholesky)/cholesky | solution.py:19
  229.5 10.0 %custom-call.29 = f32[1,128,128]{1,2,0:T(8,128)S(1)} custom-call(f32[1,128,128]{2,1,0:T(8,128)S(1)} %get-tuple-element.49), custom_call_target="InvertDiagBlocksLowerTriangular" | custom-call | tf_op jit(solution)/shard_map/jit(cholesky)/cholesky | solution.py:19
  240.1 11.7 %cholesky.343 = f32[128,128]{1,0:T(8,128)S(1)} custom-call(f32[128,128]{1,0:T(8,128)S(1)} %convolution_subtract_fusion.11), custom_call_target="Cholesky" | custom-call | tf_op jit(solution)/shard_map/jit(cholesky)/cholesky | solution.py:19
  256.5 10.6 %while.4 = (s32[]{:T(128)}, f32[512,512]{1,0:T(8,128)S(1)}, s32[4,2]{0,1:T(2,128)S(1)}, f32[4,128,128]{2,1,0:T(8,128)}, s32[]{:T(128)}) while((s32[]{:T(128)}, f32[512,512]{1,0:T(8,128)S(1)}, s32[4,2]{0,1:T(2,128)S(1)}, f32[4,128,128]{2,1,0:T(8,128)}, s32[]{:T(128)}) %tuple.73), condition=%wide.while_cond, body=%wide.while_body.sunk | while | flops 2 | bytes 132205 | solution.py:20
  267.1 40.6 %custom-call.30 = f32[4,128,128]{1,2,0:T(8,128)S(1)} custom-call(f32[4,128,128]{2,1,0:T(8,128)} %get-tuple-element.18), custom_call_target="InvertDiagBlocksLowerTriangular" | custom-call | tf_op jit(solution)/shard_map/jit(_solve_triangular)/triangular_solve | solution.py:20
  321.1 7.3 all-to-all-start
  328.5 112.4 %all-to-all-done = bf16[16,256,1024]{2,1,0:T(8,128)(2,1)} async-done(((bf16[16,256,1024]{2,1,0:T(8,128)(2,1)}), bf16[16,256,1024]{2,1,0:T(8,128)(2,1)}, u32[]{:S(2)}, u32[]{:S(2)}) %all-to-all-start) | async-done | bytes 8388640 | tf_op jit(solution)/shard_map/all_to_all | solution.py:58
  446.3 111.1 %all-reduce.4.cloned.1.call-done = bf16[2048,1024]{1,0:T(8,128)(2,1)} async-done(((bf16[2048,1024]{1,0:T(8,128)(2,1)}), bf16[2048,1024]{1,0:T(8,128)(2,1)}) %all-reduce.4.cloned.1.call-update) | async-done | bytes 4194320 | tf_op jit(solution)/shard_map/psum | solution.py:12
  557.4 23.8 %convolution_bitcast_fusion = f32[4096,1024]{0,1:T(8,128)} fusion(bf16[2048,1024]{1,0:T(8,128)(2,1)} %all-reduce.4.cloned.1.call-done, bf16[4096,2048]{1,0:T(8,128)(2,1)} %param.12), kind=kOutput, calls=%fused_computation.4 | convolution fusion | flops 17179869184 | bytes 37748736 | tf_op jit(solution)/shard_map/dot_general | solution.py:67
  581.3 95.7 %reduce-scatter.2.cloned.1.call-done = f32[256,1024]{0,1:T(8,128)} async-done(((f32[4096,1024]{0,1:T(8,128)}), f32[256,1024]{0,1:T(8,128)}) %reduce-scatter.2.cloned.1.call-update) | async-done | bytes 1048592 | tf_op jit(solution)/shard_map/reduce_scatter | solution.py:69
  683.3 150.5 %all-reduce.6.cloned.1.call-done = f32[2,512,512]{2,1,0:T(8,128)} async-done(((f32[2,512,512]{2,1,0:T(8,128)}), f32[2,512,512]{2,1,0:T(8,128)}) %all-reduce.6.cloned.1.call-update) | async-done | bytes 2097168 | tf_op jit(solution)/shard_map/psum | solution.py:86
  (118 shorter events, 90.2 us)
Async XLA Ops:
  18.6 1.0 copy-start.2
  267.1 47.4 %copy-start.1 = (f32[512,512]{1,0:T(8,128)S(1)}, f32[512,512]{1,0:T(8,128)}, u32[]{:S(2)}) copy-start(f32[512,512]{1,0:T(8,128)} %fusion.8) | copy-start | bytes 3145732
  307.7 6.8 copy-start.3
  321.1 119.8 %all-to-all-start = ((bf16[16,256,1024]{2,1,0:T(8,128)(2,1)}), bf16[16,256,1024]{2,1,0:T(8,128)(2,1)}, u32[]{:S(2)}, u32[]{:S(2)}) async-start(bf16[16,256,1024]{2,1,0:T(8,128)(2,1)} %stack.20), calls=%async_computation | async-start | bytes 16777216 | tf_op jit(solution)/shard_map/all_to_all | solution.py:58
  328.4 229.0 %all-reduce.4.cloned.1.call-start = ((), (), s32[]{:S(2)}) async-start(), calls=%async_computation.2 | async-start | bytes 8388608 | tf_op jit(solution)/shard_map/psum | solution.py:12
  446.3 230.7 %reduce-scatter.2.cloned.1.call-start = ((), (), s32[]{:S(2)}) async-start(), calls=%async_computation.3 | async-start | bytes 17825792 | tf_op jit(solution)/shard_map/reduce_scatter | solution.py:69
  581.2 252.6 %all-reduce.6.cloned.1.call-start = ((), (), s32[]{:S(2)}) async-start(), calls=%async_computation.4 | async-start | bytes 4194304 | tf_op jit(solution)/shard_map/psum | solution.py:86
  678.7 3.4 copy-start
Sparse Core Ops, SparseCore 0:
  446.4 110.9 all-reduce.3
  581.3 95.6 reduce-scatter.1
  682.4 151.3 all-reduce.5
